TPU v7x, 32 devices: a whole 2x2x4 slice. The times are simulated.
32 devices in a mesh: rows: 8 (over z, y), protos: 4 (over x, core).
Axes of the slice: x: 2, y: 2, z: 4, core: 2. Of those that a mesh axis runs over, the one named last changes fastest.
Arguments:
- features: bfloat16 [3072, 256], P('rows', 'protos'), may hold values from -12 to 12
- prototypes: bfloat16 [65536, 256], P('protos', 'rows'), may hold values from -8 to 8
- masked_index: int32 [1536], P('rows'), may hold values from 0 to 383
Outputs:
- targets: bfloat16 [1536, 65536], P('rows', 'protos')
Inputs may be any that keep to these rules, and one draw needn't show every extreme that they name: Row r of the whole takes patch (r // 192) * 384 + masked_index[r] of features.
All inputs are finite; a program needn't handle non-finite values.
Results may differ from a plain program's by a relative error of at most 0.001.
Values may be sent and summed in bfloat16 or wider, within the bound.
A program may use at most 64 MiB of HBM per device.

v0:
```python
import jax
import jax.numpy as jnp
from jax import lax
from jax.sharding import PartitionSpec as P

K = 65536
ITERS = 3
TEMP = 0.07
EPS = 1e-06


def on_device(features, prototypes, masked_index):
    chosen = jnp.take(features, masked_index, axis=0)
    patches = lax.all_gather(chosen, "protos", axis=1, tiled=True)
    feat_scale = lax.rsqrt(jnp.sum(jnp.square(patches.astype(jnp.float32)), axis=1) + EPS)
    full = lax.all_gather(prototypes, "rows", axis=1, tiled=True)
    proto_sq = jnp.sum(jnp.square(full.astype(jnp.float32)), axis=1)
    raw = lax.dot_general(
        patches, full, (((1,), (1,)), ((), ())), preferred_element_type=jnp.float32
    )
    proto_scale = lax.rsqrt(proto_sq + EPS)
    weights = jnp.exp(raw * feat_scale[:, None] * proto_scale[None, :] / TEMP)
    total_rows = masked_index.shape[0] * lax.axis_size("rows")
    row_scale = jnp.ones((patches.shape[0],), jnp.float32)
    for step in range(ITERS):
        col_part = jnp.dot(row_scale, weights, precision=lax.Precision.HIGHEST)
        col_scale = 1.0 / (K * lax.psum(col_part, "rows"))
        row_part = jnp.dot(weights, col_scale, precision=lax.Precision.HIGHEST)
        row_scale = 1.0 / (total_rows * lax.psum(row_part, "protos"))
    factor = float(K) * float(total_rows)
    return (factor * row_scale[:, None] * weights * col_scale[None, :]).astype(jnp.bfloat16)


def solution(mesh):
    in_specs = (P("rows", "protos"), P("protos", "rows"), P("rows"))
    out_specs = P("rows", "protos")
    return jax.shard_map(
        on_device, mesh=mesh, in_specs=in_specs, out_specs=out_specs, check_vma=False
    )
```

profile of v0, /device:TPU:0, one launch (start us, length us, event | category | flops | bytes accessed | tf_op | source)
XLA Modules:
  0.0 458.1 jit_solution(18258766225013638009)
XLA Ops:
  6.5 0.7 all-gather.2.cloned.1.call-update
  7.3 0.0 all-reduce.4.cloned.1.call-start
  7.3 0.9 copy.5
  8.2 0.7 compare_select_fusion
  8.9 0.8 gather_fusion
  9.7 0.7 compare_and_fusion
  10.4 0.1 broadcast_select_fusion
  10.5 0.1 copy.6
  10.6 6.5 %all_gather.6 = bf16[192,256]{0,1:T(8,128)(2,1)S(1)} all-gather(bf16[192,64]{0,1:T(8,128)(2,1)S(1)} %copy.6), channel_id=1, replica_groups=mesh['rows'=8,'protos'=4] {'protos'}, dimensions={1}, use_global_device_ids=true | all-gather | bytes 122880 | tf_op jit(solution)/shard_map/all_gather | solution.py:14
  17.1 0.1 multiply_reduce_fusion.1
  17.2 119.5 %all-gather.2.cloned.1.call-done = bf16[16384,256]{0,1:T(8,128)(2,1)} async-done(((bf16[16384,32]{0,1:T(8,128)(2,1)}), bf16[16384,256]{0,1:T(8,128)(2,1)}) %all-gather.2.cloned.1.call-update) | async-done | bytes 8388624 | tf_op jit(solution)/shard_map/all_gather | solution.py:16
  136.7 5.1 %multiply_reduce_fusion = f32[16384]{0:T(1024)S(1)} fusion(bf16[16384,256]{0,1:T(8,128)(2,1)} %all-gather.2.cloned.1.call-done), kind=kLoop, calls=%fused_computation.5 | loop fusion | flops 12566528 | bytes 8454144 | tf_op jit(solution)/shard_map/reduce_sum | solution.py:17
  141.8 5.8 %fusion.2 = f32[192,16384]{1,0:T(8,128)S(1)} fusion(bf16[192,256]{0,1:T(8,128)(2,1)S(1)} %all_gather.6, bf16[16384,256]{0,1:T(8,128)(2,1)} %all-gather.2.cloned.1.call-done, f32[16384]{0:T(1024)S(1)} %add_rsqrt_fusion, f32[192]{0:T(256)S(1)} %add_rsqrt_fusion.1), kind=kOutput, calls=%fused_computation.4 | convolution fusion | flops 1620049920 | bytes 21136128 | tf_op jit(solution)/shard_map/dot_general | solution.py:18
  147.7 4.6 copy-done
  152.2 6.6 %fusion.3 = f32[1,16384]{1,0:T(1,128)} fusion(f32[192,16384]{1,0:T(8,128)S(1)} %fusion.2), kind=kOutput, calls=%fused_computation.20 | convolution fusion | flops 37748736 | bytes 12648448 | tf_op jit(solution)/shard_map/dot_general | solution.py:26
  158.9 0.2 all-reduce.6.cloned.1.call-start
  159.1 67.3 %all-reduce.4.cloned.1.call-done = f32[16384]{0:T(1024)} async-done(((f32[16384]{0:T(1024)}), f32[16384]{0:T(1024)}) %all-reduce.4.cloned.1.call-update) | async-done | bytes 65552 | tf_op jit(solution)/shard_map/psum | solution.py:27
  226.4 0.9 multiply_divide_fusion.2
  227.3 12.7 %fusion.6 = f32[1,192]{1,0:T(1,128)S(1)} fusion(f32[192,16384]{1,0:T(8,128)} %copy-done, f32[16384,1]{0,1:T(1,128)S(1)} %bitcast.28), kind=kOutput, calls=%fused_computation.23 | convolution fusion | flops 37748736 | bytes 12649216 | tf_op jit(solution)/shard_map/dot_general | solution.py:28
  240.0 5.7 %psum.43 = f32[192]{0:T(256)S(1)} all-reduce(f32[192]{0:T(256)S(1)} %bitcast.30), channel_id=1, replica_groups=mesh['rows'=8,'protos'=4] {'protos'}, use_global_device_ids=true, to_apply=%region_3.4 | all-reduce | flops 192 | bytes 1536 | tf_op jit(solution)/shard_map/psum | solution.py:29
  245.7 9.5 %fusion.7 = f32[1,16384]{1,0:T(1,128)} fusion(f32[192,1]{0,1:T(1,128)S(1)} %bitcast.31, f32[192,16384]{1,0:T(8,128)} %copy-done), kind=kOutput, calls=%fused_computation.24 | convolution fusion | flops 37748736 | bytes 12649216 | tf_op jit(solution)/shard_map/dot_general | solution.py:26
  255.2 0.0 all-reduce.8.cloned.1.call-start
  255.3 69.6 %all-reduce.6.cloned.1.call-done = f32[16384]{0:T(1024)} async-done(((f32[16384]{0:T(1024)}), f32[16384]{0:T(1024)}) %all-reduce.6.cloned.1.call-update) | async-done | bytes 65552 | tf_op jit(solution)/shard_map/psum | solution.py:27
  324.8 0.9 multiply_divide_fusion.1
  325.7 12.7 %fusion.8 = f32[1,192]{1,0:T(1,128)S(1)} fusion(f32[192,16384]{1,0:T(8,128)} %copy-done, f32[16384,1]{0,1:T(1,128)S(1)} %bitcast.29), kind=kOutput, calls=%fused_computation.25 | convolution fusion | flops 37748736 | bytes 12649216 | tf_op jit(solution)/shard_map/dot_general | solution.py:28
  338.4 5.9 %psum.45 = f32[192]{0:T(256)S(1)} all-reduce(f32[192]{0:T(256)S(1)} %bitcast.32), channel_id=1, replica_groups=mesh['rows'=8,'protos'=4] {'protos'}, use_global_device_ids=true, to_apply=%region_5.6 | all-reduce | flops 192 | bytes 1536 | tf_op jit(solution)/shard_map/psum | solution.py:29
  344.3 9.5 %fusion.9 = f32[1,16384]{1,0:T(1,128)} fusion(f32[192,1]{0,1:T(1,128)S(1)} %bitcast.33, f32[192,16384]{1,0:T(8,128)} %copy-done), kind=kOutput, calls=%fused_computation.26 | convolution fusion | flops 37748736 | bytes 12649216 | tf_op jit(solution)/shard_map/dot_general | solution.py:26
  353.8 69.6 %all-reduce.8.cloned.1.call-done = f32[16384]{0:T(1024)} async-done(((f32[16384]{0:T(1024)}), f32[16384]{0:T(1024)}) %all-reduce.8.cloned.1.call-update) | async-done | bytes 65552 | tf_op jit(solution)/shard_map/psum | solution.py:27
  423.5 0.9 multiply_divide_fusion
  424.3 12.7 %fusion.10 = f32[1,192]{1,0:T(1,128)S(1)} fusion(f32[192,16384]{1,0:T(8,128)} %copy-done, f32[16384,1]{0,1:T(1,128)S(1)} %bitcast.24), kind=kOutput, calls=%fused_computation.27 | convolution fusion | flops 37748736 | bytes 12649216 | tf_op jit(solution)/shard_map/dot_general | solution.py:28
  437.0 5.7 %psum.47 = f32[192]{0:T(256)S(1)} all-reduce(f32[192]{0:T(256)S(1)} %bitcast.34), channel_id=1, replica_groups=mesh['rows'=8,'protos'=4] {'protos'}, use_global_device_ids=true, to_apply=%region_7.8 | all-reduce | flops 192 | bytes 1536 | tf_op jit(solution)/shard_map/psum | solution.py:29
  442.7 8.8 %multiply_convert_fusion = bf16[192,16384]{1,0:T(8,128)(2,1)} fusion(f32[192,16384]{1,0:T(8,128)} %copy-done, f32[16384]{0:T(1024)S(1)} %multiply_divide_fusion, f32[192]{0:T(256)S(1)} %divide_multiply_fusion), kind=kLoop, calls=%fused_computation.6 | loop fusion | flops 9437184 | bytes 18940672 | tf_op jit(solution)/shard_map/convert_element_type | solution.py:31
  (11 shorter events, 0.1 us)
Async XLA Ops:
  6.5 130.2 %all-gather.2.cloned.1.call-start = ((), (), s32[]{:S(2)}) async-start(), calls=%async_computation | async-start | bytes 9437184 | tf_op jit(solution)/shard_map/all_gather | solution.py:16
  7.3 219.2 %all-reduce.4.cloned.1.call-start = ((), (), s32[]{:S(2)}) async-start(), calls=%async_computation.1 | async-start | bytes 131072 | tf_op jit(solution)/shard_map/psum | solution.py:27
  147.7 4.6 copy-start
  158.9 166.0 %all-reduce.6.cloned.1.call-start = ((), (), s32[]{:S(2)}) async-start(), calls=%async_computation.2 | async-start | bytes 131072 | tf_op jit(solution)/shard_map/psum | solution.py:27
  255.2 168.3 %all-reduce.8.cloned.1.call-start = ((), (), s32[]{:S(2)}) async-start(), calls=%async_computation.3 | async-start | bytes 131072 | tf_op jit(solution)/shard_map/psum | solution.py:27
Sparse Core Ops, SparseCore 0:
  9.5 127.1 all-gather.1
  159.0 67.3 all-reduce.3
  255.3 69.4 all-reduce.5
  354.0 69.4 all-reduce.7
where the time goes:
time: 459 us; the launch traced here: 458 us
  waiting for transfers between devices  327 us (71%)
  matrix products  69.6 us (15%)
  blocking collectives  23.7 us (5%)
  other arithmetic  18.1 us (4%)
  between operations  13.2 us (3%)
  local copies, waits for them, and re-layouts  6.35 us (1%)
    psum x3, waiting for transfers between devices, on_device(): col_scale = 1.0 / (K * lax.psum(col_part, 'rows'))  207 us
    all_gather x1, waiting for transfers between devices, on_device(): full = lax.all_gather(prototypes, 'rows', axis=1, tiled=True)  120 us
    dot_general x3, matrix products, on_device(): row_part = jnp.dot(weights, col_scale, precision=lax.Precision.HIGHEST)  38.2 us
    dot_general x3, matrix products, on_device(): col_part = jnp.dot(row_scale, weights, precision=lax.Precision.HIGHEST)  25.6 us
    psum x3, blocking collectives, on_device(): row_scale = 1.0 / (total_rows * lax.psum(row_part, 'protos'))  17.2 us
  transfers between devices with their start and end apart: 4, of which 4 were waited for; matrix products, arithmetic and copies ran while one was open for 1% of the time, Pallas kernels for 0%

commit v1 on v0

--- a/solution.py
+++ b/solution.py
@@ -24,7 +24,8 @@
     row_scale = jnp.ones((patches.shape[0],), jnp.float32)
     for step in range(ITERS):
         col_part = jnp.dot(row_scale, weights, precision=lax.Precision.HIGHEST)
-        col_scale = 1.0 / (K * lax.psum(col_part, "rows"))
+        draft_yards = lambda message: lax.all_gather(message, "rows").sum(axis=0)
+        col_scale = 1.0 / (K * draft_yards(col_part))
         row_part = jnp.dot(weights, col_scale, precision=lax.Precision.HIGHEST)
         row_scale = 1.0 / (total_rows * lax.psum(row_part, "protos"))
     factor = float(K) * float(total_rows)

time: 459 us -> 344 us (0.75)
  waiting for transfers between devices: 327 us -> 120 us
  blocking collectives: 23.7 us -> 119 us
    psum x3 -> x0, waiting for transfers between devices: 207 us -> none  [on_device(): col_scale = 1.0 / (K * lax.psum(col_part, 'rows'))]
    all_gather x0 -> x3, blocking collectives: none -> 95.4 us  [on_device(): draft_yards = lambda message: lax.all_gather(message, 'rows').sum(axis=0)]
  transfers between devices with their start and end apart: 4 -> 1, of which waited for: 4 -> 1; matrix products, arithmetic and copies ran while one was open for 1% -> 1% of each run, Pallas kernels for 0% -> 0%
where the time goes in v1:
time: 344 us; the launch traced here: 343 us
  waiting for transfers between devices  120 us (35%)
  blocking collectives  119 us (35%)
  matrix products  67.7 us (20%)
  other arithmetic  16 us (5%)
  between operations  13.5 us (4%)
  local copies, waits for them, and re-layouts  6.64 us (2%)
    all_gather x1, waiting for transfers between devices, on_device(): full = lax.all_gather(prototypes, 'rows', axis=1, tiled=True)  120 us
    all_gather x3, blocking collectives, on_device(): draft_yards = lambda message: lax.all_gather(message, 'rows').sum(axis=0)  95.4 us
    dot_general x3, matrix products, on_device(): row_part = jnp.dot(weights, col_scale, precision=lax.Precision.HIGHEST)  38.2 us
    dot_general x3, matrix products, on_device(): col_part = jnp.dot(row_scale, weights, precision=lax.Precision.HIGHEST)  23.8 us
    psum x3, blocking collectives, on_device(): row_scale = 1.0 / (total_rows * lax.psum(row_part, 'protos'))  17.3 us
    convert_element_type x1, other arithmetic, on_device(): (factor * row_scale[:, None] * weights * col_scale[None, :]).astype(jnp.b...  8.83 us
  transfers between devices with their start and end apart: 1, of which 1 were waited for; matrix products, arithmetic and copies ran while one was open for 1% of the time, Pallas kernels for 0%

profile of v1, /device:TPU:0, one launch (start us, length us, event | category | flops | bytes accessed | tf_op | source)
XLA Modules:
  0.0 343.4 jit_solution(13149025408473525254)
XLA Ops:
  6.5 0.7 all-gather.5.cloned.1.call-update
  7.3 0.9 copy.7
  8.2 0.7 compare_select_fusion
  8.9 0.8 gather_fusion
  9.7 0.7 compare_and_fusion
  10.3 0.1 broadcast_select_fusion
  10.4 0.1 copy.8
  10.5 6.5 %all_gather.24 = bf16[192,256]{0,1:T(8,128)(2,1)S(1)} all-gather(bf16[192,64]{0,1:T(8,128)(2,1)S(1)} %copy.8), channel_id=1, replica_groups=mesh['rows'=8,'protos'=4] {'protos'}, dimensions={1}, use_global_device_ids=true | all-gather | bytes 122880 | tf_op jit(solution)/shard_map/all_gather | solution.py:14
  17.0 0.1 multiply_reduce_fusion.1
  17.1 119.6 %all-gather.5.cloned.1.call-done = bf16[16384,256]{0,1:T(8,128)(2,1)} async-done(((bf16[16384,32]{0,1:T(8,128)(2,1)}), bf16[16384,256]{0,1:T(8,128)(2,1)}) %all-gather.5.cloned.1.call-update) | async-done | bytes 8388624 | tf_op jit(solution)/shard_map/all_gather | solution.py:16
  136.7 5.1 %multiply_reduce_fusion = f32[16384]{0:T(1024)S(1)} fusion(bf16[16384,256]{0,1:T(8,128)(2,1)} %all-gather.5.cloned.1.call-done), kind=kLoop, calls=%fused_computation.5 | loop fusion | flops 12566528 | bytes 8454144 | tf_op jit(solution)/shard_map/reduce_sum | solution.py:17
  141.8 5.8 %fusion.2 = f32[192,16384]{1,0:T(8,128)S(1)} fusion(bf16[192,256]{0,1:T(8,128)(2,1)S(1)} %all_gather.24, bf16[16384,256]{0,1:T(8,128)(2,1)} %all-gather.5.cloned.1.call-done, f32[16384]{0:T(1024)S(1)} %add_rsqrt_fusion, f32[192]{0:T(256)S(1)} %add_rsqrt_fusion.1), kind=kOutput, calls=%fused_computation.4 | convolution fusion | flops 1620049920 | bytes 21136128 | tf_op jit(solution)/shard_map/dot_general | solution.py:18
  147.7 4.6 %copy-done = f32[192,16384]{1,0:T(8,128)} copy-done((f32[192,16384]{1,0:T(8,128)}, f32[192,16384]{1,0:T(8,128)S(1)}, u32[]{:S(2)}) %copy-start) | copy-done | bytes 12582936
  152.2 6.0 %fusion.3 = f32[1,16384]{1,0:T(1,128)S(1)} fusion(f32[192,16384]{1,0:T(8,128)S(1)} %fusion.2), kind=kOutput, calls=%fused_computation.20 | convolution fusion | flops 37748736 | bytes 12648448 | tf_op jit(solution)/shard_map/dot_general | solution.py:26
  158.2 31.8 %all-gather = f32[131072]{0:T(1024)S(1)} all-gather(f32[16384]{0:T(1024)S(1)} %bitcast.27), channel_id=2, replica_groups=mesh['rows'=8,'protos'=4] {'rows'}, dimensions={0}, use_global_device_ids=true | all-gather | bytes 589824 | tf_op jit(solution)/shard_map/all_gather | solution.py:27
  190.0 0.1 reshape.27
  190.1 0.1 reduce_sum.47
  190.2 12.7 %fusion.6 = f32[1,192]{1,0:T(1,128)S(1)} fusion(f32[192,16384]{1,0:T(8,128)} %copy-done, f32[16384,1]{0,1:T(1,128)S(1)} %bitcast.28), kind=kOutput, calls=%fused_computation.23 | convolution fusion | flops 37748736 | bytes 12649216 | tf_op jit(solution)/shard_map/dot_general | solution.py:29
  203.0 5.7 %psum.21 = f32[192]{0:T(256)S(1)} all-reduce(f32[192]{0:T(256)S(1)} %bitcast.30), channel_id=1, replica_groups=mesh['rows'=8,'protos'=4] {'protos'}, use_global_device_ids=true, to_apply=%region_3.4 | all-reduce | flops 192 | bytes 1536 | tf_op jit(solution)/shard_map/psum | solution.py:30
  208.6 8.9 %fusion.7 = f32[1,16384]{1,0:T(1,128)S(1)} fusion(f32[192,1]{0,1:T(1,128)S(1)} %bitcast.31, f32[192,16384]{1,0:T(8,128)} %copy-done), kind=kOutput, calls=%fused_computation.24 | convolution fusion | flops 37748736 | bytes 12649216 | tf_op jit(solution)/shard_map/dot_general | solution.py:26
  217.5 31.8 %all-gather.1 = f32[131072]{0:T(1024)S(1)} all-gather(f32[16384]{0:T(1024)S(1)} %bitcast.25), channel_id=3, replica_groups=mesh['rows'=8,'protos'=4] {'rows'}, dimensions={0}, use_global_device_ids=true | all-gather | bytes 589824 | tf_op jit(solution)/shard_map/all_gather | solution.py:27
  249.3 0.1 reshape.28
  249.4 0.1 reduce_sum.48
  249.6 12.7 %fusion.8 = f32[1,192]{1,0:T(1,128)S(1)} fusion(f32[192,16384]{1,0:T(8,128)} %copy-done, f32[16384,1]{0,1:T(1,128)S(1)} %bitcast.29), kind=kOutput, calls=%fused_computation.25 | convolution fusion | flops 37748736 | bytes 12649216 | tf_op jit(solution)/shard_map/dot_general | solution.py:29
  262.3 5.7 %psum.22 = f32[192]{0:T(256)S(1)} all-reduce(f32[192]{0:T(256)S(1)} %bitcast.32), channel_id=1, replica_groups=mesh['rows'=8,'protos'=4] {'protos'}, use_global_device_ids=true, to_apply=%region_5.6 | all-reduce | flops 192 | bytes 1536 | tf_op jit(solution)/shard_map/psum | solution.py:30
  268.0 8.9 %fusion.9 = f32[1,16384]{1,0:T(1,128)S(1)} fusion(f32[192,1]{0,1:T(1,128)S(1)} %bitcast.33, f32[192,16384]{1,0:T(8,128)} %copy-done), kind=kOutput, calls=%fused_computation.26 | convolution fusion | flops 37748736 | bytes 12649216 | tf_op jit(solution)/shard_map/dot_general | solution.py:26
  276.9 31.8 %all-gather.2 = f32[131072]{0:T(1024)S(1)} all-gather(f32[16384]{0:T(1024)S(1)} %bitcast.26), channel_id=4, replica_groups=mesh['rows'=8,'protos'=4] {'rows'}, dimensions={0}, use_global_device_ids=true | all-gather | bytes 589824 | tf_op jit(solution)/shard_map/all_gather | solution.py:27
  308.7 0.1 reshape.29
  308.8 0.1 reduce_sum.49
  309.0 12.7 %fusion.10 = f32[1,192]{1,0:T(1,128)S(1)} fusion(f32[192,16384]{1,0:T(8,128)} %copy-done, f32[16384,1]{0,1:T(1,128)S(1)} %bitcast.24), kind=kOutput, calls=%fused_computation.27 | convolution fusion | flops 37748736 | bytes 12649216 | tf_op jit(solution)/shard_map/dot_general | solution.py:29
  321.7 6.0 %psum.23 = f32[192]{0:T(256)S(1)} all-reduce(f32[192]{0:T(256)S(1)} %bitcast.34), channel_id=1, replica_groups=mesh['rows'=8,'protos'=4] {'protos'}, use_global_device_ids=true, to_apply=%region_7.8 | all-reduce | flops 192 | bytes 1536 | tf_op jit(solution)/shard_map/psum | solution.py:30
  327.7 8.8 %multiply_convert_fusion = bf16[192,16384]{1,0:T(8,128)(2,1)} fusion(f32[192,16384]{1,0:T(8,128)} %copy-done, f32[16384]{0:T(1024)S(1)} %multiply_divide_fusion, f32[192]{0:T(256)S(1)} %divide_multiply_fusion), kind=kLoop, calls=%fused_computation.6 | loop fusion | flops 9437184 | bytes 18940672 | tf_op jit(solution)/shard_map/convert_element_type | solution.py:32
  (11 shorter events, 0.1 us)
Async XLA Ops:
  6.5 130.2 %all-gather.5.cloned.1.call-start = ((), (), s32[]{:S(2)}) async-start(), calls=%async_computation | async-start | bytes 9437184 | tf_op jit(solution)/shard_map/all_gather | solution.py:16
  147.7 4.6 %copy-start = (f32[192,16384]{1,0:T(8,128)}, f32[192,16384]{1,0:T(8,128)S(1)}, u32[]{:S(2)}) copy-start(f32[192,16384]{1,0:T(8,128)S(1)} %fusion.2) | copy-start | bytes 37748740
Sparse Core Ops, SparseCore 0:
  9.5 127.1 all-gather.4
